TPU v7x, 32 devices: a whole 2x2x4 slice. The times are simulated.
32 devices in a mesh: groups: 2 (over x), seq: 16 (over z, y, core).
Axes of the slice: x: 2, y: 2, z: 4, core: 2. Of those that a mesh axis runs over, the one named last changes fastest.
Arguments:
- queries: bfloat16 [1024, 2048], P(('groups', 'seq')), parts along dimension 0, may hold values from -132 to 132
- fresh_keys: bfloat16 [1024, 2048], P(('groups', 'seq')), parts along dimension 0, may hold values from -6 to 6
- fresh_values: bfloat16 [1024, 2048], P(('groups', 'seq')), parts along dimension 0, may hold values from -48 to 48
- stale_keys: bfloat16 [1024, 2048], P(('groups', 'seq')), parts along dimension 0, may hold values from -6 to 6
- stale_values: bfloat16 [1024, 2048], P(('groups', 'seq')), parts along dimension 0, may hold values from -48 to 48
- patch_sizes: int32 [8], P('groups'), parts along dimension 0, may hold values from 1 to 256, 512 in all
Outputs:
- attended: bfloat16 [1024, 2048], P(('groups', 'seq')), parts along dimension 0
There are 2 independent parts, one for each index of `groups`. A program takes and returns all parts, laid end to end along the dimension named above; each array names one. Nothing has to cross between parts.
Inputs may be any that keep to these rules, and one draw needn't show every extreme that they name: `patch_sizes`: the patch lengths sum to 512.
All inputs are finite; a program needn't handle non-finite values.
Results may differ from a plain program's by a relative error of at most 0.006.
Values may be sent and summed in bfloat16 or wider, within the bound.
A program may use at most 64 MiB of HBM per device.

v0:
```python
import jax
import jax.numpy as jnp
from jax import lax
from jax.sharding import PartitionSpec as P

H = 16


def shifted(block, axis, distance):
    devices = range(lax.axis_size(axis))
    route = [((i - distance) % len(devices), i) for i in devices]
    return lax.ppermute(block, axis, route)


def shards(queries, fresh_keys, fresh_values, stale_keys, stale_values, patch_sizes):
    local_rows, columns = queries.shape
    head_size = columns // H
    devices = lax.axis_size("seq")
    query_groups = devices // H
    sub_rows = local_rows // query_groups
    shape_in = (sub_rows, devices, head_size)
    moved = (
        lax.all_to_all(queries.reshape(shape_in), "seq", split_axis=1, concat_axis=0, tiled=True),
        lax.all_to_all(
            fresh_keys.reshape(shape_in), "seq", split_axis=1, concat_axis=0, tiled=True
        ),
        lax.all_to_all(
            fresh_values.reshape(shape_in), "seq", split_axis=1, concat_axis=0, tiled=True
        ),
        lax.all_to_all(
            stale_keys.reshape(shape_in), "seq", split_axis=1, concat_axis=0, tiled=True
        ),
        lax.all_to_all(
            stale_values.reshape(shape_in), "seq", split_axis=1, concat_axis=0, tiled=True
        ),
    )
    query_rows = moved[0].reshape(-1, head_size)
    stacked = jnp.stack(
        [
            moved[1].reshape(-1, head_size),
            moved[2].reshape(-1, head_size),
            moved[3].reshape(-1, head_size),
            moved[4].reshape(-1, head_size),
        ]
    )
    own_group = lax.axis_index("seq") // H
    patch_ends = jnp.cumsum(patch_sizes)[:-1]
    positions = (
        jnp.arange(devices, dtype=jnp.int32)[:, None] * local_rows
        + jnp.arange(sub_rows, dtype=jnp.int32)[None, :] * query_groups
    ).reshape(-1)

    def patch_of(group):
        hits = positions[:, None] + group >= patch_ends[None, :]
        return jnp.sum(hits.astype(jnp.int32), axis=1)

    score_scale = head_size ** (-0.5)
    contract = (((1,), (1,)), ((), ()))
    query_patch = patch_of(own_group)

    def absorb(carry_state, key_block, source_group):
        running_max, denominator, numerator = carry_state
        is_fresh = patch_of(source_group)[None, :] <= query_patch[:, None]
        fresh_scores = lax.dot_general(
            query_rows, key_block[0], contract, preferred_element_type=jnp.float32
        )
        stale_scores = lax.dot_general(
            query_rows, key_block[2], contract, preferred_element_type=jnp.float32
        )
        scores = jnp.where(is_fresh, fresh_scores, stale_scores) * score_scale
        new_max = jnp.maximum(running_max, jnp.max(scores, axis=1, keepdims=True))
        rescale = jnp.exp(running_max - new_max)
        weights = jnp.exp(scores - new_max)
        denominator = denominator * rescale + jnp.sum(weights, axis=1, keepdims=True)
        rounded = weights.astype(jnp.bfloat16)
        zeroes = jnp.zeros_like(rounded)
        numerator = numerator * rescale + jnp.dot(
            jnp.where(is_fresh, rounded, zeroes), key_block[1], preferred_element_type=jnp.float32
        )
        numerator = numerator + jnp.dot(
            jnp.where(is_fresh, zeroes, rounded), key_block[3], preferred_element_type=jnp.float32
        )
        return (new_max, denominator, numerator)

    query_count = query_rows.shape[0]
    carry_state = (
        jnp.full((query_count, 1), -1e30, jnp.float32),
        jnp.zeros((query_count, 1), jnp.float32),
        jnp.zeros((query_count, head_size), jnp.float32),
    )
    carry_state = absorb(carry_state, stacked, own_group)
    travelling = stacked
    for offset in range(1, query_groups):
        travelling = shifted(travelling, "seq", H)
        carry_state = absorb(carry_state, travelling, (own_group - offset) % query_groups)
    attended = (carry_state[2] / carry_state[1]).astype(jnp.bfloat16)
    returned = lax.all_to_all(
        attended.reshape(devices, sub_rows, 1, head_size),
        "seq",
        split_axis=0,
        concat_axis=2,
        tiled=True,
    )
    return returned.reshape(local_rows, columns)


def solution(mesh):
    in_specs = (
        P(("groups", "seq"), None),
        P(("groups", "seq"), None),
        P(("groups", "seq"), None),
        P(("groups", "seq"), None),
        P(("groups", "seq"), None),
        P("groups"),
    )
    out_specs = P(("groups", "seq"), None)
    return jax.shard_map(shards, mesh=mesh, in_specs=in_specs, out_specs=out_specs, check_vma=False)
```

profile of v0, /device:TPU:0, one launch (start us, length us, event | category | flops | bytes accessed | tf_op | source)
XLA Modules:
  0.0 74.3 jit_solution(5553754712294257362)
XLA Ops:
  0.0 0.0 copy-start
  0.0 0.9 %copy-done = bf16[32,2048]{1,0:T(8,128)(2,1)S(1)} copy-done((bf16[32,2048]{1,0:T(8,128)(2,1)S(1)}, bf16[32,2048]{1,0:T(8,128)(2,1)}, u32[]{:S(2)}) %copy-start) | copy-done | bytes 131096
  0.9 0.7 copy_bitcast_fusion.5
  1.6 0.0 copy-start.1
  1.6 7.5 %all-to-all-start = ((bf16[32,16,128]{2,0,1:T(8,128)(2,1)}), bf16[32,16,128]{2,0,1:T(8,128)(2,1)S(1)}, u32[]{:S(2)}, u32[]{:S(2)}) async-start(bf16[32,16,128]{2,0,1:T(8,128)(2,1)} %copy_bitcast_fusion.5), calls=%async_computation | async-start | bytes 262144 | tf_op jit(solution)/shard_map/all_to_all | solution.py:23
  9.2 0.0 copy-start.5
  9.2 0.6 copy-done.5
  9.8 0.2 reduce-window.4
  10.0 0.0 copy-done.1
  10.0 0.0 copy-start.2
  10.0 0.7 copy_bitcast_fusion.4
  10.7 0.3 copy-done.2
  10.9 0.0 copy-start.3
  10.9 0.7 copy_bitcast_fusion.3
  11.6 0.1 add_add_fusion
  11.7 0.1 add.55
  11.8 0.1 copy-done.3
  11.9 0.7 copy_bitcast_fusion.2
  12.6 0.0 copy-start.4
  12.6 4.5 %all-to-all-done = bf16[32,16,128]{2,0,1:T(8,128)(2,1)S(1)} async-done(((bf16[32,16,128]{2,0,1:T(8,128)(2,1)}), bf16[32,16,128]{2,0,1:T(8,128)(2,1)S(1)}, u32[]{:S(2)}, u32[]{:S(2)}) %all-to-all-start) | async-done | bytes 131104 | tf_op jit(solution)/shard_map/all_to_all | solution.py:23
  17.0 3.5 %all-to-all-start.1 = ((bf16[32,16,128]{2,0,1:T(8,128)(2,1)}), bf16[32,16,128]{2,0,1:T(8,128)(2,1)S(1)}, u32[]{:S(2)}, u32[]{:S(2)}) async-start(bf16[32,16,128]{2,0,1:T(8,128)(2,1)} %copy_bitcast_fusion.4), calls=%async_computation.1 | async-start | bytes 262144 | tf_op jit(solution)/shard_map/all_to_all | solution.py:24
  20.6 0.1 convert_reduce_fusion
  20.6 0.0 copy-done.4
  20.6 0.7 copy_bitcast_fusion.1
  21.3 7.1 %all-to-all-done.1 = bf16[32,16,128]{2,0,1:T(8,128)(2,1)S(1)} async-done(((bf16[32,16,128]{2,0,1:T(8,128)(2,1)}), bf16[32,16,128]{2,0,1:T(8,128)(2,1)S(1)}, u32[]{:S(2)}, u32[]{:S(2)}) %all-to-all-start.1) | async-done | bytes 131104 | tf_op jit(solution)/shard_map/all_to_all | solution.py:24
  28.4 3.5 %all-to-all-start.2 = ((bf16[32,16,128]{2,0,1:T(8,128)(2,1)}), bf16[32,16,128]{2,0,1:T(8,128)(2,1)S(1)}, u32[]{:S(2)}, u32[]{:S(2)}) async-start(bf16[32,16,128]{2,0,1:T(8,128)(2,1)} %copy_bitcast_fusion.3), calls=%async_computation.2 | async-start | bytes 262144 | tf_op jit(solution)/shard_map/all_to_all | solution.py:30
  31.9 0.3 fusion.17
  32.2 7.6 %all-to-all-done.2 = bf16[32,16,128]{2,0,1:T(8,128)(2,1)S(1)} async-done(((bf16[32,16,128]{2,0,1:T(8,128)(2,1)}), bf16[32,16,128]{2,0,1:T(8,128)(2,1)S(1)}, u32[]{:S(2)}, u32[]{:S(2)}) %all-to-all-start.2) | async-done | bytes 131104 | tf_op jit(solution)/shard_map/all_to_all | solution.py:30
  39.8 3.5 %all-to-all-start.3 = ((bf16[32,16,128]{2,0,1:T(8,128)(2,1)}), bf16[32,16,128]{2,0,1:T(8,128)(2,1)S(1)}, u32[]{:S(2)}, u32[]{:S(2)}) async-start(bf16[32,16,128]{2,0,1:T(8,128)(2,1)} %copy_bitcast_fusion.2), calls=%async_computation.3 | async-start | bytes 262144 | tf_op jit(solution)/shard_map/all_to_all | solution.py:27
  43.3 0.3 fusion.16
  43.7 0.2 fusion.3
  43.9 7.3 %all-to-all-done.3 = bf16[32,16,128]{2,0,1:T(8,128)(2,1)S(1)} async-done(((bf16[32,16,128]{2,0,1:T(8,128)(2,1)}), bf16[32,16,128]{2,0,1:T(8,128)(2,1)S(1)}, u32[]{:S(2)}, u32[]{:S(2)}) %all-to-all-start.3) | async-done | bytes 131104 | tf_op jit(solution)/shard_map/all_to_all | solution.py:27
  51.2 3.5 %all-to-all-start.4 = ((bf16[32,16,128]{2,0,1:T(8,128)(2,1)}), bf16[32,16,128]{2,0,1:T(8,128)(2,1)S(1)}, u32[]{:S(2)}, u32[]{:S(2)}) async-start(bf16[32,16,128]{2,0,1:T(8,128)(2,1)} %copy_bitcast_fusion.1), calls=%async_computation.4 | async-start | bytes 262144 | tf_op jit(solution)/shard_map/all_to_all | solution.py:33
  54.7 0.4 convolution_add_fusion.1
  55.2 7.4 %all-to-all-done.4 = bf16[32,16,128]{2,0,1:T(8,128)(2,1)S(1)} async-done(((bf16[32,16,128]{2,0,1:T(8,128)(2,1)}), bf16[32,16,128]{2,0,1:T(8,128)(2,1)S(1)}, u32[]{:S(2)}, u32[]{:S(2)}) %all-to-all-start.4) | async-done | bytes 131104 | tf_op jit(solution)/shard_map/all_to_all | solution.py:33
  62.6 0.5 fusion.2
  63.1 10.5 %all_to_all.90 = bf16[16,32,1,128]{3,1,2,0:T(8,128)(2,1)S(1)} all-to-all(bf16[16,32,1,128]{3,1,2,0:T(8,128)(2,1)S(1)} %bitcast.79), channel_id=1, replica_groups=mesh['groups'=2,'seq'=16] {'seq'}, dimensions={0} | all-to-all | bytes 262144 | tf_op jit(solution)/shard_map/all_to_all | solution.py:97
  73.6 0.1 copy.34
  73.6 0.7 copy.47
  (4 shorter events, 0.0 us)
Async XLA Ops:
  0.0 0.9 %copy-start = (bf16[32,2048]{1,0:T(8,128)(2,1)S(1)}, bf16[32,2048]{1,0:T(8,128)(2,1)}, u32[]{:S(2)}) copy-start(bf16[32,2048]{1,0:T(8,128)(2,1)} %param.6) | copy-start | bytes 393220
  1.6 8.4 %copy-start.1 = (bf16[32,2048]{1,0:T(8,128)(2,1)S(1)}, bf16[32,2048]{1,0:T(8,128)(2,1)}, u32[]{:S(2)}) copy-start(bf16[32,2048]{1,0:T(8,128)(2,1)} %param.7) | copy-start | bytes 393220
  1.6 15.5 %all-to-all-start = ((bf16[32,16,128]{2,0,1:T(8,128)(2,1)}), bf16[32,16,128]{2,0,1:T(8,128)(2,1)S(1)}, u32[]{:S(2)}, u32[]{:S(2)}) async-start(bf16[32,16,128]{2,0,1:T(8,128)(2,1)} %copy_bitcast_fusion.5), calls=%async_computation | async-start | bytes 262144 | tf_op jit(solution)/shard_map/all_to_all | solution.py:23
  9.2 0.7 copy-start.5
  10.0 1.0 %copy-start.2 = (bf16[32,2048]{1,0:T(8,128)(2,1)S(1)}, bf16[32,2048]{1,0:T(8,128)(2,1)}, u32[]{:S(2)}) copy-start(bf16[32,2048]{1,0:T(8,128)(2,1)} %param.9) | copy-start | bytes 393220
  10.9 1.0 %copy-start.3 = (bf16[32,2048]{1,0:T(8,128)(2,1)S(1)}, bf16[32,2048]{1,0:T(8,128)(2,1)}, u32[]{:S(2)}) copy-start(bf16[32,2048]{1,0:T(8,128)(2,1)} %param.8) | copy-start | bytes 393220
  12.6 8.1 %copy-start.4 = (bf16[32,2048]{1,0:T(8,128)(2,1)S(1)}, bf16[32,2048]{1,0:T(8,128)(2,1)}, u32[]{:S(2)}) copy-start(bf16[32,2048]{1,0:T(8,128)(2,1)} %param.10) | copy-start | bytes 393220
  17.0 11.4 %all-to-all-start.1 = ((bf16[32,16,128]{2,0,1:T(8,128)(2,1)}), bf16[32,16,128]{2,0,1:T(8,128)(2,1)S(1)}, u32[]{:S(2)}, u32[]{:S(2)}) async-start(bf16[32,16,128]{2,0,1:T(8,128)(2,1)} %copy_bitcast_fusion.4), calls=%async_computation.1 | async-start | bytes 262144 | tf_op jit(solution)/shard_map/all_to_all | solution.py:24
  28.4 11.4 %all-to-all-start.2 = ((bf16[32,16,128]{2,0,1:T(8,128)(2,1)}), bf16[32,16,128]{2,0,1:T(8,128)(2,1)S(1)}, u32[]{:S(2)}, u32[]{:S(2)}) async-start(bf16[32,16,128]{2,0,1:T(8,128)(2,1)} %copy_bitcast_fusion.3), calls=%async_computation.2 | async-start | bytes 262144 | tf_op jit(solution)/shard_map/all_to_all | solution.py:30
  39.8 11.4 %all-to-all-start.3 = ((bf16[32,16,128]{2,0,1:T(8,128)(2,1)}), bf16[32,16,128]{2,0,1:T(8,128)(2,1)S(1)}, u32[]{:S(2)}, u32[]{:S(2)}) async-start(bf16[32,16,128]{2,0,1:T(8,128)(2,1)} %copy_bitcast_fusion.2), calls=%async_computation.3 | async-start | bytes 262144 | tf_op jit(solution)/shard_map/all_to_all | solution.py:27
  51.2 11.4 %all-to-all-start.4 = ((bf16[32,16,128]{2,0,1:T(8,128)(2,1)}), bf16[32,16,128]{2,0,1:T(8,128)(2,1)S(1)}, u32[]{:S(2)}, u32[]{:S(2)}) async-start(bf16[32,16,128]{2,0,1:T(8,128)(2,1)} %copy_bitcast_fusion.1), calls=%async_computation.4 | async-start | bytes 262144 | tf_op jit(solution)/shard_map/all_to_all | solution.py:33
where the time goes:
time: 74.9 us; the launch traced here: 74.3 us
  waiting for transfers between devices  33.9 us (45%)
  starting transfers between devices  21.6 us (29%)
  blocking collectives  10.5 us (14%)
  local copies, waits for them, and re-layouts  6.15 us (8%)
  matrix products  1.53 us (2%)
    all_to_all x1, blocking collectives, shards(): lax.all_to_all(attended.reshape(devices, sub_rows, 1, head_size), 'seq',...  10.5 us
    all_to_all x1, waiting for transfers between devices, shards(): lax.all_to_all(stale_keys.reshape(shape_in), 'seq', split_axis=1, concat_...  7.57 us
    all_to_all x1, starting transfers between devices, shards(): lax.all_to_all(queries.reshape(shape_in), 'seq', split_axis=1, concat_axi...  7.55 us
    all_to_all x1, waiting for transfers between devices, shards(): lax.all_to_all(stale_values.reshape(shape_in), 'seq', split_axis=1, conca...  7.43 us
    all_to_all x1, waiting for transfers between devices, shards(): lax.all_to_all(fresh_values.reshape(shape_in), 'seq', split_axis=1, conca...  7.33 us
    all_to_all x1, waiting for transfers between devices, shards(): lax.all_to_all(fresh_keys.reshape(shape_in), 'seq', split_axis=1, concat_...  7.11 us
    all_to_all x1, waiting for transfers between devices, shards(): lax.all_to_all(queries.reshape(shape_in), 'seq', split_axis=1, concat_axi...  4.46 us
    all_to_all x1, starting transfers between devices, shards(): lax.all_to_all(fresh_values.reshape(shape_in), 'seq', split_axis=1, conca...  3.51 us
  transfers between devices with their start and end apart: 5, of which 5 were waited for; matrix products, arithmetic and copies ran while one was open for 6% of the time, Pallas kernels for 0%

commit v1 on v0

v1 whole, which is shorter than its diff:
```python
import functools

import jax
import jax.numpy as jnp
from jax import lax
from jax.experimental import pallas as pl
from jax.experimental.pallas import tpu as pltpu
from jax.sharding import PartitionSpec as P

H = 16
MESH = pl.DeviceIdType.MESH


def each(count, body):
    if count <= 32:
        for k in range(1, count):
            body(k)
    else:
        lax.fori_loop(1, count, lambda k, c: (body(k), c)[1], 0)


def flipped(me, k, count):
    if count & (count - 1):
        return lax.rem(me + k, count)
    peer, bit = 0, 1
    while bit < count:
        peer = peer + bit * lax.rem(me // bit + k // bit, 2)
        bit *= 2
    return peer


def kernel(
    n, q_ref, fk_ref, sk_ref, fv_ref, sv_ref, sizes_ref, out_ref,
    stage, got_q, got_k, got_v, att, wf_s, ws_s,
    load_sem, own_sem, send_sem, recv_sem, back_send, back_recv,
):
    rows, columns = q_ref.shape
    hd = columns // H
    me = lax.axis_index("seq")
    head = lax.rem(me, H)
    base = me - head
    keys = n * rows
    queries = H * rows

    loads = []
    for i, ref in enumerate((q_ref, fk_ref, sk_ref, fv_ref, sv_ref)):
        c = pltpu.make_async_copy(ref, stage.at[i], load_sem.at[i])
        c.start()
        loads.append(c)

    barrier = pltpu.get_barrier_semaphore()
    each(n, lambda k: pl.semaphore_signal(
        barrier, inc=1, device_id={"seq": flipped(me, k, n)}, device_id_type=MESH))
    pl.semaphore_wait(barrier, n - 1)

    def cols(h):
        return pl.ds(pl.multiple_of(h * hd, hd), hd)

    def at(p):
        return pl.ds(pl.multiple_of(p * rows, rows), rows)

    def views(phase, peer_head, source):
        if phase == 0:
            return stage.at[0, :, cols(peer_head)], got_q.at[at(lax.rem(source, H)), :]
        if phase == 1:
            return stage.at[1:3, :, cols(peer_head)], got_k.at[:, at(source), :]
        return stage.at[3:5, :, cols(peer_head)], got_v.at[:, at(source), :]

    def remote(phase, peer, source, slot):
        src, dst = views(phase, lax.rem(peer, H), source)
        return pltpu.make_async_remote_copy(
            src_ref=src, dst_ref=dst,
            send_sem=send_sem.at[phase, slot], recv_sem=recv_sem.at[phase, slot],
            device_id={"seq": peer}, device_id_type=MESH)

    def own(phase):
        src, dst = views(phase, head, me)
        return pltpu.make_async_copy(src, dst, own_sem.at[phase])

    for phase, needs in ((0, (0,)), (1, (1, 2)), (2, (3, 4))):
        for i in needs:
            loads[i].wait()

        each(H if phase == 0 else n, (lambda k: remote(
            0, base + flipped(head, H - k, H), me, H - k).start()) if phase == 0 else (
            lambda k: remote(phase, flipped(me, n - k, n), me, n - k).start()))
        own(phase).start()

    def arrived(phase, count):
        each(count, lambda k: remote(phase, me, me, k).wait_recv())
        own(phase).wait()

    arrived(0, H)
    arrived(1, n)

    ends, total = [], 0
    for p in range(sizes_ref.shape[0] - 1):
        total = total + sizes_ref[p]
        ends.append(total)

    block = 4 * rows
    scale = hd ** (-0.5)
    contract = (((1,), (1,)), ((), ()))

    def score(b):
        at_b = pl.ds(pl.multiple_of(b * block, block), block)
        token = base * rows + b * block + lax.broadcasted_iota(jnp.int32, (block, 1), 0)
        limit = jnp.full((block, 1), keys, jnp.int32)
        for e in reversed(ends):
            limit = jnp.where(token < e, e, limit)
        fresh = lax.broadcasted_iota(jnp.int32, (block, keys), 1) < limit
        qb = got_q[at_b, :]
        sf = lax.dot_general(qb, got_k[0], contract, preferred_element_type=jnp.float32)
        ss = lax.dot_general(qb, got_k[1], contract, preferred_element_type=jnp.float32)
        s = jnp.where(fresh, sf, ss)
        w = jnp.exp((s - jnp.max(s, axis=1, keepdims=True)) * scale)
        den = jnp.sum(w, axis=1, keepdims=True)
        zero = jnp.zeros_like(w)
        wf_s[at_b, :] = jnp.where(fresh, w, zero).astype(jnp.bfloat16)
        ws_s[at_b, :] = jnp.where(fresh, zero, w).astype(jnp.bfloat16)
        return den

    blocks = queries // block
    dens = [score(b) for b in range(blocks)]

    arrived(2, n)

    def back(j, slot):
        return pltpu.make_async_remote_copy(
            src_ref=att.at[at(j), :], dst_ref=out_ref.at[:, cols(head)],
            send_sem=back_send.at[j], recv_sem=back_recv.at[slot],
            device_id={"seq": base + j}, device_id_type=MESH)

    def back_own(j):
        return pltpu.make_async_copy(att.at[at(j), :], out_ref.at[:, cols(head)], own_sem.at[3])

    for b in range(blocks):
        at_b = pl.ds(b * block, block)
        num = jnp.dot(wf_s[at_b, :], got_v[0], preferred_element_type=jnp.float32)
        num = num + jnp.dot(ws_s[at_b, :], got_v[1], preferred_element_type=jnp.float32)
        att[at_b, :] = (num / dens[b]).astype(jnp.bfloat16)
        for j in range(4 * b, 4 * b + 4):
            pl.when(head != j)(lambda j=j: back(j, head).start())
            pl.when(head == j)(lambda j=j: back_own(j).start())

    each(H, lambda k: remote(0, me, me, k).wait_send())
    each(n, lambda k: remote(1, me, me, k).wait_send())
    each(n, lambda k: remote(2, me, me, k).wait_send())
    for j in range(H):
        @pl.when(head != j)
        def _(j=j):
            back(j, j).wait()
    back_own(0).wait()


def shards(queries, fresh_keys, fresh_values, stale_keys, stale_values, patch_sizes):
    rows, columns = queries.shape
    n = lax.axis_size("seq")
    hd = columns // H
    keys, count = n * rows, H * rows
    dma = pltpu.SemaphoreType.DMA
    any_spec = pl.BlockSpec(memory_space=pl.ANY)
    return pl.pallas_call(
        functools.partial(kernel, n),
        out_shape=jax.ShapeDtypeStruct((rows, columns), queries.dtype),
        in_specs=[any_spec] * 5 + [pl.BlockSpec(memory_space=pltpu.SMEM)],
        out_specs=any_spec,
        scratch_shapes=[
            pltpu.VMEM((5, rows, columns), queries.dtype),
            pltpu.VMEM((count, hd), queries.dtype),
            pltpu.VMEM((2, keys, hd), queries.dtype),
            pltpu.VMEM((2, keys, hd), queries.dtype),
            pltpu.VMEM((count, hd), queries.dtype),
            pltpu.VMEM((count, keys), queries.dtype),
            pltpu.VMEM((count, keys), queries.dtype),
            dma((5,)), dma((4,)), dma((3, n)), dma((3, n)), dma((H,)), dma((H,)),
        ],
        compiler_params=pltpu.CompilerParams(collective_id=0, has_side_effects=True),
    )(queries, fresh_keys, stale_keys, fresh_values, stale_values, patch_sizes)


def solution(mesh):
    spec = P(("groups", "seq"), None)
    return jax.shard_map(
        shards, mesh=mesh, in_specs=(spec,) * 5 + (P("groups"),), out_specs=spec, check_vma=False)
```

time: 74.9 us -> 30.3 us (0.40)
  waiting for transfers between devices: 33.9 us -> 0 us
  Pallas kernels: 0 us -> 28.6 us
  starting transfers between devices: 21.6 us -> 0 us
  blocking collectives: 10.5 us -> 0 us
  local copies, waits for them, and re-layouts: 6.15 us -> 1.57 us
  matrix products: 1.53 us -> 0 us
    all_to_all x5 -> x0, waiting for transfers between devices: 33.9 us -> none  [the longest x1 7.57 us: shards(): lax.all_to_all(stale_keys.reshape(shape_in), 'seq', split_axis=1, concat_...]
    pallas_call x0 -> x1, Pallas kernels: none -> 28.6 us  [shards(): pl.pallas_call(functools.partial(kernel, n), out_shape=jax.ShapeDtypeStru...]
    all_to_all x5 -> x0, starting transfers between devices: 21.6 us -> none  [the longest x1 7.55 us: shards(): lax.all_to_all(queries.reshape(shape_in), 'seq', split_axis=1, concat_axi...]
    all_to_all x1 -> x0, blocking collectives: 10.5 us -> none  [shards(): lax.all_to_all(attended.reshape(devices, sub_rows, 1, head_size), 'seq',...]
    reshape x5 -> x0, local copies, waits for them, and re-layouts: 3.36 us -> none  [the longest x1 0.68 us: shards(): fresh_values.reshape(shape_in)]
    dot_general x4 -> x0, matrix products: 1.53 us -> none  [the longest x1 0.47 us: absorb(): jnp.dot(jnp.where(is_fresh, zeroes, rounded), key_block[3], preferred_ele...]
    unnamed x13 -> x1, local copies, waits for them, and re-layouts: 2.66 us -> 1.57 us
  transfers between devices with their start and end apart: 5 -> 0, of which waited for: 5 -> 0; matrix products, arithmetic and copies ran while one was open for 6% -> 0% of each run, Pallas kernels for 0% -> 0%
where the time goes in v1:
time: 30.3 us; the launch traced here: 30.1 us
  Pallas kernels  28.6 us (94%)
  local copies, waits for them, and re-layouts  1.57 us (5%)
    pallas_call x1, Pallas kernels, shards(): pl.pallas_call(functools.partial(kernel, n), out_shape=jax.ShapeDtypeStru...  28.6 us
    unnamed x1, local copies, waits for them, and re-layouts  1.57 us

profile of v1, /device:TPU:0, one launch (start us, length us, event | category | flops | bytes accessed | tf_op | source)
XLA Modules:
  0.0 30.1 jit_solution(14363364488721013470)
XLA Ops:
  0.0 28.6 %shard_map.64 = bf16[32,2048]{1,0:T(8,128)(2,1)} custom-call(bf16[32,2048]{1,0:T(8,128)(2,1)} %q_ref.1, bf16[32,2048]{1,0:T(8,128)(2,1)} %fk_ref.1, bf16[32,2048]{1,0:T(8,128)(2,1)} %sk_ref.1, bf16[32,2048]{1,0:T(8,128)(2,1)} %fv_ref.1, bf16[32,2048]{1,0:T(8,128)(2,1)} %sv_ref.1, s32[4]{0:T(128)} %sizes_ref.1), custom_call_target="tpu_custom_call" | custom-call | tf_op jit(solution)/shard_map/pallas_call | solution.py:163
  28.6 1.6 %copy.8 = bf16[32,2048]{1,0:T(8,128)(2,1)} copy(bf16[32,2048]{1,0:T(8,128)(2,1)} %shard_map.64) | data formatting | bytes 262144

commit v2 on v1

--- a/solution.py
+++ b/solution.py
@@ -81,9 +81,10 @@
         for i in needs:
             loads[i].wait()
 
-        each(H if phase == 0 else n, (lambda k: remote(
-            0, base + flipped(head, H - k, H), me, H - k).start()) if phase == 0 else (
-            lambda k: remote(phase, flipped(me, n - k, n), me, n - k).start()))
+        if phase == 0:
+            each(H, lambda k: remote(0, base + flipped(head, k, H), me, k).start())
+        else:
+            each(n, lambda k: remote(phase, flipped(me, k, n), me, k).start())
         own(phase).start()
 
     def arrived(phase, count):
@@ -120,37 +121,37 @@
         ws_s[at_b, :] = jnp.where(fresh, zero, w).astype(jnp.bfloat16)
         return den
 
-    blocks = queries // block
-    dens = [score(b) for b in range(blocks)]
+    order = [flipped(head // 4, k, H // 4) for k in (2, 1, 3, 0)]
+    dens = [score(b) for b in order]
 
     arrived(2, n)
 
-    def back(j, slot):
+    def back(slot):
+        j = flipped(head, slot, H)
         return pltpu.make_async_remote_copy(
             src_ref=att.at[at(j), :], dst_ref=out_ref.at[:, cols(head)],
-            send_sem=back_send.at[j], recv_sem=back_recv.at[slot],
+            send_sem=back_send.at[slot], recv_sem=back_recv.at[slot],
             device_id={"seq": base + j}, device_id_type=MESH)
 
-    def back_own(j):
-        return pltpu.make_async_copy(att.at[at(j), :], out_ref.at[:, cols(head)], own_sem.at[3])
+    back_own = pltpu.make_async_copy(att.at[at(head), :], out_ref.at[:, cols(head)], own_sem.at[3])
 
-    for b in range(blocks):
-        at_b = pl.ds(b * block, block)
+    for i, k in enumerate((2, 1, 3, 0)):
+        at_b = pl.ds(pl.multiple_of(order[i] * block, block), block)
         num = jnp.dot(wf_s[at_b, :], got_v[0], preferred_element_type=jnp.float32)
         num = num + jnp.dot(ws_s[at_b, :], got_v[1], preferred_element_type=jnp.float32)
-        att[at_b, :] = (num / dens[b]).astype(jnp.bfloat16)
-        for j in range(4 * b, 4 * b + 4):
-            pl.when(head != j)(lambda j=j: back(j, head).start())
-            pl.when(head == j)(lambda j=j: back_own(j).start())
+        att[at_b, :] = (num / dens[i]).astype(jnp.bfloat16)
+        for slot in range(4 * k, 4 * k + 4):
+            if slot:
+                back(slot).start()
+            else:
+                back_own.start()
 
     each(H, lambda k: remote(0, me, me, k).wait_send())
     each(n, lambda k: remote(1, me, me, k).wait_send())
     each(n, lambda k: remote(2, me, me, k).wait_send())
-    for j in range(H):
-        @pl.when(head != j)
-        def _(j=j):
-            back(j, j).wait()
-    back_own(0).wait()
+    for slot in range(1, H):
+        back(slot).wait()
+    back_own.wait()
 
 
 def shards(queries, fresh_keys, fresh_values, stale_keys, stale_values, patch_sizes):
@@ -162,9 +163,9 @@
     any_spec = pl.BlockSpec(memory_space=pl.ANY)
     return pl.pallas_call(
         functools.partial(kernel, n),
-        out_shape=jax.ShapeDtypeStruct((rows, columns), queries.dtype),
+        out_shape=pltpu.VMEM((rows, columns), queries.dtype),
         in_specs=[any_spec] * 5 + [pl.BlockSpec(memory_space=pltpu.SMEM)],
-        out_specs=any_spec,
+        out_specs=pl.BlockSpec(memory_space=pltpu.VMEM),
         scratch_shapes=[
             pltpu.VMEM((5, rows, columns), queries.dtype),
             pltpu.VMEM((count, hd), queries.dtype),

time: 30.3 us -> 30 us (0.990)
  local copies, waits for them, and re-layouts: 1.57 us -> 0.66 us
  Pallas kernels: 28.6 us -> 29.1 us
    unnamed x1, local copies, waits for them, and re-layouts: 1.57 us -> 0.66 us
    pallas_call x1, Pallas kernels: 28.6 us -> 29.1 us  [shards(): pl.pallas_call(functools.partial(kernel, n), out_shape=pltpu.VMEM((rows,...]
where the time goes in v2:
time: 30 us; the launch traced here: 29.8 us
  Pallas kernels  29.1 us (97%)
  local copies, waits for them, and re-layouts  0.66 us (2%)
    pallas_call x1, Pallas kernels, shards(): pl.pallas_call(functools.partial(kernel, n), out_shape=pltpu.VMEM((rows,...  29.1 us
    unnamed x1, local copies, waits for them, and re-layouts  0.66 us

profile of v2, /device:TPU:0, one launch (start us, length us, event | category | flops | bytes accessed | tf_op | source)
XLA Modules:
  0.0 29.8 jit_solution(8270503024039365392)
XLA Ops:
  0.0 29.1 %shard_map.64 = bf16[32,2048]{1,0:T(8,128)(2,1)S(1)} custom-call(bf16[32,2048]{1,0:T(8,128)(2,1)} %q_ref.1, bf16[32,2048]{1,0:T(8,128)(2,1)} %fk_ref.1, bf16[32,2048]{1,0:T(8,128)(2,1)} %sk_ref.1, bf16[32,2048]{1,0:T(8,128)(2,1)} %fv_ref.1, bf16[32,2048]{1,0:T(8,128)(2,1)} %sv_ref.1, s32[4]{0:T(128)} %sizes_ref.1), custom_call_target="tpu_custom_call" | custom-call | tf_op jit(solution)/shard_map/pallas_call | solution.py:164
  29.2 0.7 %copy.8 = bf16[32,2048]{1,0:T(8,128)(2,1)} copy(bf16[32,2048]{1,0:T(8,128)(2,1)S(1)} %shard_map.64) | data formatting | bytes 262144

commit v3 on v2

v3 whole, which is shorter than its diff:
```python
import functools

import jax
import jax.numpy as jnp
from jax import lax
from jax.experimental import pallas as pl
from jax.experimental.pallas import tpu as pltpu
from jax.sharding import PartitionSpec as P

H = 16
MESH = pl.DeviceIdType.MESH


def each(count, body):
    if count <= 32:
        for k in range(1, count):
            body(k)
    else:
        lax.fori_loop(1, count, lambda k, c: (body(k), c)[1], 0)


def flipped(me, k, count):
    if count & (count - 1):
        return lax.rem(me + k, count)
    peer, bit = 0, 1
    while bit < count:
        peer = peer + bit * lax.rem(me // bit + k // bit, 2)
        bit *= 2
    return peer


def kernel(
    n, fk_ref, sk_ref, fv_ref, sv_ref, q_ref, sizes_ref, out_ref,
    stage, got_q, got_kv, att,
    load_sem, own_sem, send_sem, recv_sem, back_send, back_recv,
):
    rows, columns = q_ref.shape
    hd = columns // H
    me = lax.axis_index("seq")
    head = lax.rem(me, H)
    base = me - head
    keys = n * rows
    queries = H * rows

    loads = []
    for i, ref in enumerate((fk_ref, sk_ref, fv_ref, sv_ref, q_ref)):
        c = pltpu.make_async_copy(ref, stage.at[i], load_sem.at[i])
        c.start()
        loads.append(c)

    barrier = pltpu.get_barrier_semaphore()
    each(n, lambda k: pl.semaphore_signal(
        barrier, inc=1, device_id={"seq": flipped(me, k, n)}, device_id_type=MESH))
    pl.semaphore_wait(barrier, n - 1)

    def cols(h):
        return pl.ds(pl.multiple_of(h * hd, hd), hd)

    def at(p):
        return pl.ds(pl.multiple_of(p * rows, rows), rows)

    def views(phase, peer_head, source):
        if phase == 0:
            return stage.at[0:4, :, cols(peer_head)], got_kv.at[:, at(source), :]
        return stage.at[4, :, cols(peer_head)], got_q.at[at(lax.rem(source, H)), :]

    def remote(phase, peer, source, slot):
        src, dst = views(phase, lax.rem(peer, H), source)
        return pltpu.make_async_remote_copy(
            src_ref=src, dst_ref=dst,
            send_sem=send_sem.at[phase, slot], recv_sem=recv_sem.at[phase, slot],
            device_id={"seq": peer}, device_id_type=MESH)

    def own(phase):
        src, dst = views(phase, head, me)
        return pltpu.make_async_copy(src, dst, own_sem.at[phase])

    for i in range(4):
        loads[i].wait()
    each(n, lambda k: remote(0, flipped(me, k, n), me, k).start())
    own(0).start()
    loads[4].wait()
    each(H, lambda k: remote(1, base + flipped(head, k, H), me, k).start())
    own(1).start()

    ends, total = [], 0
    for p in range(sizes_ref.shape[0] - 1):
        total = total + sizes_ref[p]
        ends.append(total)

    block = 4 * rows
    scale = hd ** (-0.5)
    contract = (((1,), (1,)), ((), ()))

    def attend(b):
        at_b = pl.ds(pl.multiple_of(b * block, block), block)
        token = base * rows + b * block + lax.broadcasted_iota(jnp.int32, (block, 1), 0)
        limit = jnp.full((block, 1), keys, jnp.int32)
        for e in reversed(ends):
            limit = jnp.where(token < e, e, limit)
        fresh = lax.broadcasted_iota(jnp.int32, (block, keys), 1) < limit
        qb = got_q[at_b, :]
        sf = lax.dot_general(qb, got_kv[0], contract, preferred_element_type=jnp.float32)
        ss = lax.dot_general(qb, got_kv[1], contract, preferred_element_type=jnp.float32)
        s = jnp.where(fresh, sf, ss)
        w = jnp.exp((s - jnp.max(s, axis=1, keepdims=True)) * scale)
        den = jnp.sum(w, axis=1, keepdims=True)
        zero = jnp.zeros_like(w)
        wf = jnp.where(fresh, w, zero).astype(jnp.bfloat16)
        ws = jnp.where(fresh, zero, w).astype(jnp.bfloat16)
        num = jnp.dot(wf, got_kv[2], preferred_element_type=jnp.float32)
        num = num + jnp.dot(ws, got_kv[3], preferred_element_type=jnp.float32)
        att[at_b, :] = (num / den).astype(jnp.bfloat16)

    def back(slot):
        j = flipped(head, slot, H)
        return pltpu.make_async_remote_copy(
            src_ref=att.at[at(j), :], dst_ref=out_ref.at[:, cols(head)],
            send_sem=back_send.at[slot], recv_sem=back_recv.at[slot],
            device_id={"seq": base + j}, device_id_type=MESH)

    back_own = pltpu.make_async_copy(att.at[at(head), :], out_ref.at[:, cols(head)], own_sem.at[2])

    each(n, lambda k: remote(0, me, me, k).wait_recv())
    own(0).wait()
    for k in range(H // 4):
        for slot in range(4 * k, 4 * k + 4):
            if slot:
                remote(1, me, me, slot).wait_recv()
            else:
                own(1).wait()
        attend(flipped(head // 4, k, H // 4))
        for slot in range(4 * k, 4 * k + 4):
            if slot:
                back(slot).start()
            else:
                back_own.start()

    each(n, lambda k: remote(0, me, me, k).wait_send())
    each(H, lambda k: remote(1, me, me, k).wait_send())
    for slot in range(1, H):
        back(slot).wait()
    back_own.wait()


def shards(queries, fresh_keys, fresh_values, stale_keys, stale_values, patch_sizes):
    rows, columns = queries.shape
    n = lax.axis_size("seq")
    hd = columns // H
    keys, count = n * rows, H * rows
    dma = pltpu.SemaphoreType.DMA
    any_spec = pl.BlockSpec(memory_space=pl.ANY)
    return pl.pallas_call(
        functools.partial(kernel, n),
        out_shape=pltpu.VMEM((rows, columns), queries.dtype),
        in_specs=[any_spec] * 5 + [pl.BlockSpec(memory_space=pltpu.SMEM)],
        out_specs=pl.BlockSpec(memory_space=pltpu.VMEM),
        scratch_shapes=[
            pltpu.VMEM((5, rows, columns), queries.dtype),
            pltpu.VMEM((count, hd), queries.dtype),
            pltpu.VMEM((4, keys, hd), queries.dtype),
            pltpu.VMEM((count, hd), queries.dtype),
            dma((5,)), dma((3,)), dma((2, n)), dma((2, n)), dma((H,)), dma((H,)),
        ],
        compiler_params=pltpu.CompilerParams(collective_id=0, has_side_effects=True),
    )(fresh_keys, stale_keys, fresh_values, stale_values, queries, patch_sizes)


def solution(mesh):
    spec = P(("groups", "seq"), None)
    return jax.shard_map(
        shards, mesh=mesh, in_specs=(spec,) * 5 + (P("groups"),), out_specs=spec, check_vma=False)
```

time: 30 us -> 30 us (level)
  no operation moved by 1% of the time
where the time goes in v3:
time: 30 us; the launch traced here: 29.9 us
  Pallas kernels  29.2 us (97%)
  local copies, waits for them, and re-layouts  0.66 us (2%)
    pallas_call x1, Pallas kernels, shards(): pl.pallas_call(functools.partial(kernel, n), out_shape=pltpu.VMEM((rows,...  29.2 us
    unnamed x1, local copies, waits for them, and re-layouts  0.66 us

profile of v3, /device:TPU:0, one launch (start us, length us, event | category | flops | bytes accessed | tf_op | source)
XLA Modules:
  0.0 29.9 jit_solution(15029782674897863625)
XLA Ops:
  0.0 29.2 %shard_map.64 = bf16[32,2048]{1,0:T(8,128)(2,1)S(1)} custom-call(bf16[32,2048]{1,0:T(8,128)(2,1)} %fk_ref.1, bf16[32,2048]{1,0:T(8,128)(2,1)} %sk_ref.1, bf16[32,2048]{1,0:T(8,128)(2,1)} %fv_ref.1, bf16[32,2048]{1,0:T(8,128)(2,1)} %sv_ref.1, bf16[32,2048]{1,0:T(8,128)(2,1)} %q_ref.1, s32[4]{0:T(128)} %sizes_ref.1), custom_call_target="tpu_custom_call" | custom-call | tf_op jit(solution)/shard_map/pallas_call | solution.py:153
  29.2 0.7 %copy.8 = bf16[32,2048]{1,0:T(8,128)(2,1)} copy(bf16[32,2048]{1,0:T(8,128)(2,1)S(1)} %shard_map.64) | data formatting | bytes 262144

commit v4 on v3

--- a/solution.py
+++ b/solution.py
@@ -75,13 +75,13 @@
         src, dst = views(phase, head, me)
         return pltpu.make_async_copy(src, dst, own_sem.at[phase])
 
+    loads[4].wait()
+    each(H, lambda k: remote(1, base + flipped(head, k, H), me, k).start())
+    own(1).start()
     for i in range(4):
         loads[i].wait()
     each(n, lambda k: remote(0, flipped(me, k, n), me, k).start())
     own(0).start()
-    loads[4].wait()
-    each(H, lambda k: remote(1, base + flipped(head, k, H), me, k).start())
-    own(1).start()
 
     ends, total = [], 0
     for p in range(sizes_ref.shape[0] - 1):
@@ -123,7 +123,7 @@
 
     each(n, lambda k: remote(0, me, me, k).wait_recv())
     own(0).wait()
-    for k in range(H // 4):
+    for k in (2, 3, 1, 0):
         for slot in range(4 * k, 4 * k + 4):
             if slot:
                 remote(1, me, me, slot).wait_recv()

time: 30 us -> 29.2 us (0.973)
  Pallas kernels: 29.2 us -> 28.4 us
    pallas_call x1, Pallas kernels: 29.2 us -> 28.4 us  [shards(): pl.pallas_call(functools.partial(kernel, n), out_shape=pltpu.VMEM((rows,...]
where the time goes in v4:
time: 29.2 us; the launch traced here: 29.1 us
  Pallas kernels  28.4 us (97%)
  local copies, waits for them, and re-layouts  0.66 us (2%)
    pallas_call x1, Pallas kernels, shards(): pl.pallas_call(functools.partial(kernel, n), out_shape=pltpu.VMEM((rows,...  28.4 us
    unnamed x1, local copies, waits for them, and re-layouts  0.66 us

profile of v4, /device:TPU:0, one launch (start us, length us, event | category | flops | bytes accessed | tf_op | source)
XLA Modules:
  0.0 29.1 jit_solution(5799988589896840714)
XLA Ops:
  0.0 28.4 %shard_map.64 = bf16[32,2048]{1,0:T(8,128)(2,1)S(1)} custom-call(bf16[32,2048]{1,0:T(8,128)(2,1)} %fk_ref.1, bf16[32,2048]{1,0:T(8,128)(2,1)} %sk_ref.1, bf16[32,2048]{1,0:T(8,128)(2,1)} %fv_ref.1, bf16[32,2048]{1,0:T(8,128)(2,1)} %sv_ref.1, bf16[32,2048]{1,0:T(8,128)(2,1)} %q_ref.1, s32[4]{0:T(128)} %sizes_ref.1), custom_call_target="tpu_custom_call" | custom-call | tf_op jit(solution)/shard_map/pallas_call | solution.py:153
  28.4 0.7 %copy.8 = bf16[32,2048]{1,0:T(8,128)(2,1)} copy(bf16[32,2048]{1,0:T(8,128)(2,1)S(1)} %shard_map.64) | data formatting | bytes 262144

commit v5 on v4

--- a/solution.py
+++ b/solution.py
@@ -32,7 +32,7 @@
 def kernel(
     n, fk_ref, sk_ref, fv_ref, sv_ref, q_ref, sizes_ref, out_ref,
     stage, got_q, got_kv, att,
-    load_sem, own_sem, send_sem, recv_sem, back_send, back_recv,
+    load_sem, own_sem, send_sem, recv_sem, back_send, back_recv, here,
 ):
     rows, columns = q_ref.shape
     hd = columns // H
@@ -48,11 +48,6 @@
         c.start()
         loads.append(c)
 
-    barrier = pltpu.get_barrier_semaphore()
-    each(n, lambda k: pl.semaphore_signal(
-        barrier, inc=1, device_id={"seq": flipped(me, k, n)}, device_id_type=MESH))
-    pl.semaphore_wait(barrier, n - 1)
-
     def cols(h):
         return pl.ds(pl.multiple_of(h * hd, hd), hd)
 
@@ -75,12 +70,50 @@
         src, dst = views(phase, head, me)
         return pltpu.make_async_copy(src, dst, own_sem.at[phase])
 
-    loads[4].wait()
-    each(H, lambda k: remote(1, base + flipped(head, k, H), me, k).start())
+    quarter = n // 4
+    half = n // 2
+    lane = me // quarter
+    inner = lax.rem(lane + 1, 4) >= 2
+    like = [k for k in range(1, n) if k // quarter in (0, 3)]
+    cross = [k for k in range(1, n) if k // quarter in (1, 2)]
+    barrier = pltpu.get_barrier_semaphore()
+
+    def greet(sem, ks):
+        for k in ks:
+            pl.semaphore_signal(
+                sem, inc=1, device_id={"seq": flipped(me, k, n)}, device_id_type=MESH)
+
+    def send(ks):
+        for k in ks:
+            if k < H:
+                remote(1, flipped(me, k, n), me, k).start()
+        for k in ks:
+            remote(0, flipped(me, k, n), me, k).start()
+
+    def loaded():
+        for load in loads:
+            load.wait()
+
+    @pl.when(inner)
+    def _():
+        greet(barrier, like + cross)
+        pl.semaphore_wait(barrier, half - 1)
+        loaded()
+        send(like)
+        pl.semaphore_wait(here, half)
+        greet(here, [quarter])
+        send(cross)
+
+    @pl.when(jnp.logical_not(inner))
+    def _():
+        pl.semaphore_wait(barrier, half)
+        greet(here, cross)
+        loaded()
+        send(cross)
+        pl.semaphore_wait(here, 1)
+        send(like)
+
     own(1).start()
-    for i in range(4):
-        loads[i].wait()
-    each(n, lambda k: remote(0, flipped(me, k, n), me, k).start())
     own(0).start()
 
     ends, total = [], 0
@@ -160,7 +193,7 @@
             pltpu.VMEM((count, hd), queries.dtype),
             pltpu.VMEM((4, keys, hd), queries.dtype),
             pltpu.VMEM((count, hd), queries.dtype),
-            dma((5,)), dma((3,)), dma((2, n)), dma((2, n)), dma((H,)), dma((H,)),
+            dma((5,)), dma((3,)), dma((2, n)), dma((2, n)), dma((H,)), dma((H,)), pltpu.SemaphoreType.REGULAR,
         ],
         compiler_params=pltpu.CompilerParams(collective_id=0, has_side_effects=True),
     )(fresh_keys, stale_keys, fresh_values, stale_values, queries, patch_sizes)

time: 29.2 us -> 29.6 us (1.014)
  Pallas kernels: 28.4 us -> 28.8 us
    pallas_call x1, Pallas kernels: 28.4 us -> 28.8 us  [shards(): pl.pallas_call(functools.partial(kernel, n), out_shape=pltpu.VMEM((rows,...]
where the time goes in v5:
time: 29.6 us; the launch traced here: 29.4 us
  Pallas kernels  28.8 us (97%)
  local copies, waits for them, and re-layouts  0.66 us (2%)
    pallas_call x1, Pallas kernels, shards(): pl.pallas_call(functools.partial(kernel, n), out_shape=pltpu.VMEM((rows,...  28.8 us
    unnamed x1, local copies, waits for them, and re-layouts  0.66 us

profile of v5, /device:TPU:0, one launch (start us, length us, event | category | flops | bytes accessed | tf_op | source)
XLA Modules:
  0.0 29.4 jit_solution(7830058579865922719)
XLA Ops:
  0.0 28.8 %shard_map.64 = bf16[32,2048]{1,0:T(8,128)(2,1)S(1)} custom-call(bf16[32,2048]{1,0:T(8,128)(2,1)} %fk_ref.1, bf16[32,2048]{1,0:T(8,128)(2,1)} %sk_ref.1, bf16[32,2048]{1,0:T(8,128)(2,1)} %fv_ref.1, bf16[32,2048]{1,0:T(8,128)(2,1)} %sv_ref.1, bf16[32,2048]{1,0:T(8,128)(2,1)} %q_ref.1, s32[4]{0:T(128)} %sizes_ref.1), custom_call_target="tpu_custom_call" | custom-call | tf_op jit(solution)/shard_map/pallas_call | solution.py:186
  28.8 0.7 %copy.8 = bf16[32,2048]{1,0:T(8,128)(2,1)} copy(bf16[32,2048]{1,0:T(8,128)(2,1)S(1)} %shard_map.64) | data formatting | bytes 262144
